TPU v7x, 128 devices: a whole 4x4x4 slice. The times are simulated.
128 devices in a mesh: rows: 16 (over x, y_lo, core), dim: 8 (over y_hi, z).
Axes of the slice: x: 4, y: 4 (y_hi: 2, y_lo: 2; y = y_hi * 2 + y_lo), z: 4, core: 2. Of those that a mesh axis runs over, the one named last changes fastest.
Arguments:
- entity_table: float32 [524288, 512], P(('rows', 'dim')), may hold values from -2.5 to 2.5
- relations: float32 [822, 512], replicated, may hold values from -6 to 6
- thresholds: float32 [64], replicated, may hold values from 0.2 to 2
- head_ids: int32 [2048], replicated, may hold values from 0 to 524287
- rel_ids: int32 [2048], replicated, may hold values from 0 to 821
- thr_idx: int32 [2048], replicated, may hold values from 0 to 63
Outputs:
- serving_table: float32 [524288, 512], P('rows', 'dim')
- fraction: float32 [2048], P(('rows', 'dim'))
All inputs are finite; a program needn't handle non-finite values.
Results may differ from a plain program's by a relative error of at most 0.0011.
Values sent between devices are 32-bit elements; how exact they have to be, the bound alone decides.
No kernel may reach another device: no remote copies, remote signals or barrier semaphores. Data moves between devices by JAX's collectives and lax.ppermute only.
A program may use at most 128 MiB of HBM per device.

v0:
```python
import jax
import jax.numpy as jnp
from jax import lax
from jax.sharding import PartitionSpec as P

sharpness = 2.0


def cut_along(value, dim, length):
    lengths = value.shape
    parts = value.reshape(*lengths[:dim], length, lengths[dim] // length, *lengths[dim + 1 :])
    return jnp.moveaxis(parts, dim, 0)


def cut_rows(length, count):
    lap = length // count
    if lap >= 8:
        lap -= lap % 8
    return [lap * k for k in range(1, count)]


def joined_along(parts, dim):
    lengths = list(parts.shape[1:])
    lengths[dim] *= parts.shape[0]
    return jnp.moveaxis(parts, 0, dim).reshape(lengths)


def several_exchanges(value, axis, pieces, split_dim, concat_dim):
    parts = cut_along(value, split_dim, lax.axis_size(axis))
    cut = max(range(1, max(2, parts.ndim - 1)), key=lambda d: parts.shape[d])
    outs = []
    for slab in jnp.split(parts, cut_rows(parts.shape[cut], pieces), axis=cut):
        if slab.size:
            outs.append(lax.all_to_all(slab, axis, split_axis=0, concat_axis=0, tiled=True))
    return joined_along(jnp.concatenate(outs, axis=cut), concat_dim)


def pick_rows(table, head_ids, start):
    count = table.shape[0]
    local = head_ids - start
    owned = (local >= 0) & (local < count)
    picked = jnp.take(table, jnp.clip(local, 0, count - 1), axis=0)
    return jnp.where(owned[:, None], picked, jnp.zeros_like(picked))


def shards(entity_table, relations, thresholds, head_ids, rel_ids, thr_idx):
    local_rows = entity_table.shape[0]
    width = entity_table.shape[1]
    total_ents = local_rows * lax.axis_size("rows") * lax.axis_size("dim")
    serving = several_exchanges(entity_table, "dim", 2, 1, 0)
    start = (lax.axis_index("rows") * lax.axis_size("dim") + lax.axis_index("dim")) * local_rows
    partial_value = pick_rows(entity_table, head_ids, start)
    head_vecs = lax.psum(partial_value, ("rows", "dim"))
    query = (head_vecs * jnp.take(relations, rel_ids, axis=0)).astype(jnp.bfloat16)
    ent_low = entity_table.astype(jnp.bfloat16)
    level = jnp.take(thresholds, thr_idx)
    queries = query.shape[0]
    query_blocks = query.reshape(queries // 512, 512, width)
    level_blocks = level.reshape(queries // 512, 512)

    def score_block(pair):
        rows_q, rows_level = pair
        score = jnp.dot(rows_q, ent_low.T, preferred_element_type=jnp.float32)
        soft = jax.nn.sigmoid(sharpness * (score - rows_level[:, None]))
        return jnp.sum(soft, axis=1) * (1.0 / total_ents)

    partial_share = lax.map(score_block, (query_blocks, level_blocks)).reshape(queries)
    fraction = lax.psum_scatter(partial_share, ("rows", "dim"), scatter_dimension=0, tiled=True)
    return (serving, fraction)


def solution(mesh):
    placed = (P(("rows", "dim"), None), P(), P(), P(), P(), P())
    return jax.shard_map(
        shards,
        mesh=mesh,
        in_specs=placed,
        out_specs=(P("rows", "dim"), P(("rows", "dim"))),
        check_vma=False,
    )
```

profile of v0, /device:TPU:1, one launch (start us, length us, event | category | flops | bytes accessed | tf_op | source)
XLA Modules:
  0.0 349.4 jit_solution(9521090022698641144)
XLA Ops:
  7.2 0.0 copy-start
  7.2 9.0 %copy.12 = f32[4096,512]{0,1:T(8,128)} copy(f32[4096,512]{1,0:T(8,128)} %param.8) | data formatting | bytes 16777216 | tf_op args[0]
  16.2 7.9 %fusion.6 = (f32[8,2048,64]{1,2,0:T(8,128)}, f32[8,2048,64]{1,2,0:T(8,128)}) fusion(f32[8,4096,64]{1,2,0:T(8,128)} %bitcast.87), kind=kLoop, calls=%fused_computation.21 | loop fusion | bytes 16777216 | tf_op jit(solution)/shard_map/split | solution.py:32
  24.1 0.0 copy-start.4
  24.1 8.6 %all-to-all-start = ((f32[8,2048,64]{1,2,0:T(8,128)}), f32[8,2048,64]{1,2,0:T(8,128)}, u32[]{:S(2)}, u32[]{:S(2)}) async-start(f32[8,2048,64]{1,2,0:T(8,128)} %get-tuple-element.40), calls=%async_computation | async-start | bytes 8388608 | tf_op jit(solution)/shard_map/all_to_all | solution.py:34
  32.7 0.0 all-reduce.3.cloned.1.call-start
  32.7 0.0 copy-done.4
  32.8 12.9 %gather_fusion = f32[2048,512]{1,0:T(8,128)} fusion(f32[4096,512]{1,0:T(8,128)} %param.8, s32[2048]{0:T(1024)S(1)} %fusion.5), kind=kCustom, calls=%fused_computation | custom fusion | bytes 8396800 | tf_op jit(solution)/shard_map/jit(_take)/gather | solution.py:42
  45.7 4.0 %select_select_fusion = f32[2048,512]{1,0:T(8,128)} fusion(f32[2048,512]{1,0:T(8,128)} %gather_fusion, pred[2048]{0:T(1024)(128)(4,1)S(1)} %get-tuple-element.43, pred[2048]{0:T(1024)(128)(4,1)S(1)} %get-tuple-element.42), kind=kLoop, calls=%fused_computation.11 | loop fusion | flops 2097152 | bytes 8392704 | tf_op jit(solution)/shard_map/jit(_where)/select_n | solution.py:43
  49.6 0.0 all-reduce.3.cloned.1.call-update
  49.7 0.0 copy-start.2
  49.7 0.0 copy-start.5
  49.7 0.0 copy-start.3
  49.7 5.9 %convert_element_type.7 = bf16[4096,512]{1,0:T(8,128)(2,1)} convert(f32[4096,512]{1,0:T(8,128)} %param.8) | non-fusion elementwise | flops 2097152 | bytes 12582912 | tf_op jit(solution)/shard_map/convert_element_type | solution.py:55
  55.5 0.0 copy-done.2
  55.5 0.7 fusion.10
  56.2 0.7 fusion.8
  57.0 0.7 fusion.7
  57.7 0.7 fusion.9
  58.4 0.0 copy-done.5
  58.4 39.7 %select_select_fusion.1 = f32[2048]{0:T(1024)S(1)} fusion(s32[2048]{0:T(1024)S(1)} %copy-done.5, f32[]{:T(128)} %bitcast.7, f32[]{:T(128)} %bitcast.8, f32[]{:T(128)} %bitcast.9, f32[]{:T(128)} %bitcast.10, f32[]{:T(128)} %bitcast.11, f32[]{:T(128)} %bitcast.12, f32[]{:T(128)} %bitcast.13, f32[]{:T(128)} %bitcast.14, f32[]{:T(128)} %bitcast.15, f32[]{:T(128)} %bitcast.16, ...), kind=kLoop, calls=%fused_computation.15 | loop fusion | flops 272384 | bytes 16640 | tf_op jit(solution)/shard_map/jit(_take)/select_n | solution.py:56
  98.2 0.0 copy-done.3
  98.2 0.0 copy-done
  98.2 8.9 %gather_fusion.1 = f32[2048,512]{1,0:T(8,128)} fusion(f32[822,512]{1,0:T(8,128)S(1)} %copy-done, s32[2048]{0:T(1024)S(1)} %fusion.4), kind=kCustom, calls=%fused_computation.1 | custom fusion | bytes 8396800 | tf_op jit(solution)/shard_map/jit(_take)/gather | solution.py:54
  107.1 112.8 %all-reduce.3.cloned.1.call-done = f32[2048,512]{1,0:T(8,128)} async-done(((f32[2048,512]{1,0:T(8,128)}), f32[2048,512]{1,0:T(8,128)}) %all-reduce.3.cloned.1.call-update) | async-done | bytes 4194320 | tf_op jit(solution)/shard_map/psum | solution.py:53
  219.9 4.7 %multiply_convert_fusion = bf16[2048,512]{1,0:T(8,128)(2,1)} fusion(f32[2048,512]{1,0:T(8,128)} %all-reduce.3.cloned.1.call-done, f32[2048,512]{1,0:T(8,128)} %gather_fusion.1, pred[2048]{0:T(1024)(128)(4,1)S(1)} %compare_and_fusion), kind=kLoop, calls=%fused_computation.10 | loop fusion | flops 3145728 | bytes 10487808 | tf_op jit(solution)/shard_map/convert_element_type | solution.py:54
  224.6 0.0 all-to-all-done
  224.6 4.7 %all-to-all-start.1 = ((f32[8,2048,64]{1,2,0:T(8,128)}), f32[8,2048,64]{1,2,0:T(8,128)}, u32[]{:S(2)}, u32[]{:S(2)}) async-start(f32[8,2048,64]{1,2,0:T(8,128)} %get-tuple-element.41), calls=%async_computation.1 | async-start | bytes 8388608 | tf_op jit(solution)/shard_map/all_to_all | solution.py:34
  229.4 22.9 %while.10 = (s32[]{:T(128)}, f32[4,512]{1,0:T(4,128)S(1)}, bf16[4,512,512]{2,1,0:T(8,128)(2,1)}, bf16[4096,512]{1,0:T(8,128)(2,1)}, f32[4,512]{1,0:T(4,128)S(1)}, /*index=5*/s32[]{:T(128)}, s32[]{:T(128)}) while((s32[]{:T(128)}, f32[4,512]{1,0:T(4,128)S(1)}, bf16[4,512,512]{2,1,0:T(8,128)(2,1)}, bf16[4096,512]{1,0:T(8,128)(2,1)}, ...), condition=%wide.region_3.4_spmd, body=%wide.region_1.3_spmd.sunk | while | flops 2160066560 | bytes 4735073 | solution.py:67
  229.4 5.6 %fusion.17 = f32[512]{0:T(512)S(1)} fusion(bf16[4096,512]{1,0:T(8,128)(2,1)} %get-tuple-element.156, f32[512]{0:T(512)S(1)} %bitcast.91, bf16[4,512,512]{2,1,0:T(8,128)(2,1)} %get-tuple-element.155, s32[]{:T(128)S(6)} %copy.20), kind=kOutput, calls=%fused_computation.3.clone.1 | convolution fusion | flops 2160066048 | bytes 4722692 | tf_op jit(solution)/shard_map/while/body/eval_jaxpr/dot_general | solution.py:63
  235.1 0.1 dynamic_update_slice.5
  235.1 5.6 %fusion.17 = f32[512]{0:T(512)S(1)} fusion(bf16[4096,512]{1,0:T(8,128)(2,1)} %get-tuple-element.156, f32[512]{0:T(512)S(1)} %bitcast.91, bf16[4,512,512]{2,1,0:T(8,128)(2,1)} %get-tuple-element.155, s32[]{:T(128)S(6)} %copy.20), kind=kOutput, calls=%fused_computation.3.clone.1 | convolution fusion | flops 2160066048 | bytes 4722692 | tf_op jit(solution)/shard_map/while/body/eval_jaxpr/dot_general | solution.py:63
  240.8 0.1 dynamic_update_slice.5
  240.9 5.6 %fusion.17 = f32[512]{0:T(512)S(1)} fusion(bf16[4096,512]{1,0:T(8,128)(2,1)} %get-tuple-element.156, f32[512]{0:T(512)S(1)} %bitcast.91, bf16[4,512,512]{2,1,0:T(8,128)(2,1)} %get-tuple-element.155, s32[]{:T(128)S(6)} %copy.20), kind=kOutput, calls=%fused_computation.3.clone.1 | convolution fusion | flops 2160066048 | bytes 4722692 | tf_op jit(solution)/shard_map/while/body/eval_jaxpr/dot_general | solution.py:63
  246.5 0.1 dynamic_update_slice.5
  246.6 5.6 %fusion.17 = f32[512]{0:T(512)S(1)} fusion(bf16[4096,512]{1,0:T(8,128)(2,1)} %get-tuple-element.156, f32[512]{0:T(512)S(1)} %bitcast.91, bf16[4,512,512]{2,1,0:T(8,128)(2,1)} %get-tuple-element.155, s32[]{:T(128)S(6)} %copy.20), kind=kOutput, calls=%fused_computation.3.clone.1 | convolution fusion | flops 2160066048 | bytes 4722692 | tf_op jit(solution)/shard_map/while/body/eval_jaxpr/dot_general | solution.py:63
  252.3 0.1 dynamic_update_slice.5
  252.4 81.6 %all-reduce = f32[2048]{0:T(1024)S(1)} all-reduce(f32[2048]{0:T(1024)S(1)} %bitcast.92), channel_id=2, replica_groups=mesh['rows'=16,'dim'=8] {'rows','dim'}, use_global_device_ids=true, to_apply=%region_4.5.clone | all-reduce | flops 2048 | bytes 16384
  334.0 0.6 dynamic-slice
  334.6 0.0 all-to-all-done.1
  334.6 4.0 %maximum_bitcast_fusion = f32[8,8,8,4096]{3,2,1,0:T(8,128)S(1)} fusion(f32[8,2048,64]{1,2,0:T(8,128)} %all-to-all-done.1, f32[8,2048,64]{1,2,0:T(8,128)} %all-to-all-done), kind=kLoop, calls=%fused_computation.9 | loop fusion | flops 2097152 | bytes 16777216
  338.6 0.0 copy-start.1
  338.6 3.9 %copy.14 = f32[8,8,8,4096]{3,2,0,1:T(8,128)} copy(f32[8,8,8,4096]{3,2,1,0:T(8,128)S(1)} %maximum_bitcast_fusion) | data formatting | bytes 16777216 | tf_op jit(solution)/shard_map/reshape | solution.py:25
  342.5 0.0 copy-done.1
  (15 shorter events, 0.1 us)
Async XLA Ops:
  7.2 91.0 %copy-start = (f32[822,512]{1,0:T(8,128)S(1)}, f32[822,512]{1,0:T(8,128)}, u32[]{:S(2)}) copy-start(f32[822,512]{1,0:T(8,128)} %param.9) | copy-start | bytes 5050372
  24.1 8.7 %copy-start.4 = (s32[2048]{0:T(1024)S(1)}, s32[2048]{0:T(1024)}, u32[]{:S(2)}) copy-start(s32[2048]{0:T(1024)} %param.11) | copy-start | bytes 24580
  24.1 200.6 %all-to-all-start = ((f32[8,2048,64]{1,2,0:T(8,128)}), f32[8,2048,64]{1,2,0:T(8,128)}, u32[]{:S(2)}, u32[]{:S(2)}) async-start(f32[8,2048,64]{1,2,0:T(8,128)} %get-tuple-element.40), calls=%async_computation | async-start | bytes 8388608 | tf_op jit(solution)/shard_map/all_to_all | solution.py:34
  32.7 187.2 %all-reduce.3.cloned.1.call-start = ((), (), s32[]{:S(2)}) async-start(), calls=%async_computation.2 | async-start | bytes 8388608 | tf_op jit(solution)/shard_map/psum | solution.py:53
  49.7 5.9 %copy-start.2 = (f32[64]{0:T(128)S(1)}, f32[64]{0:T(128)}, u32[]{:S(2)}) copy-start(f32[64]{0:T(128)} %param.10) | copy-start | bytes 772
  49.7 8.7 %copy-start.5 = (s32[2048]{0:T(1024)S(1)}, s32[2048]{0:T(1024)}, u32[]{:S(2)}) copy-start(s32[2048]{0:T(1024)} %param.13) | copy-start | bytes 24580
  49.7 48.5 %copy-start.3 = (s32[2048]{0:T(1024)S(1)}, s32[2048]{0:T(1024)}, u32[]{:S(2)}) copy-start(s32[2048]{0:T(1024)} %param.12) | copy-start | bytes 24580
  224.6 109.9 %all-to-all-start.1 = ((f32[8,2048,64]{1,2,0:T(8,128)}), f32[8,2048,64]{1,2,0:T(8,128)}, u32[]{:S(2)}, u32[]{:S(2)}) async-start(f32[8,2048,64]{1,2,0:T(8,128)} %get-tuple-element.41), calls=%async_computation.1 | async-start | bytes 8388608 | tf_op jit(solution)/shard_map/all_to_all | solution.py:34
  338.6 4.0 %copy-start.1 = (f32[822,512]{1,0:T(8,128)S(1)}, f32[822,512]{1,0:T(8,128)}, u32[]{:S(2)}) copy-start(f32[822,512]{1,0:T(8,128)} %param.9) | copy-start | bytes 5050372
Sparse Core Ops, SparseCore 0:
  49.8 170.1 all-reduce.2
where the time goes:
time: 351 us; the launch traced here: 349 us
  waiting for transfers between devices  113 us (32%)
  blocking collectives  81.6 us (23%)
  other arithmetic  58.3 us (17%)
  local copies, waits for them, and re-layouts  46.3 us (13%)
  matrix products  22.6 us (6%)
  between operations  14.2 us (4%)
  starting transfers between devices  13.4 us (4%)
    psum x1, waiting for transfers between devices, shards(): head_vecs = lax.psum(partial_value, ('rows', 'dim'))  113 us
    unnamed x1, blocking collectives  81.6 us
    select_n x1, other arithmetic, shards(): level = jnp.take(thresholds, thr_idx)  39.7 us
    dot_general x4, matrix products, score_block(): score = jnp.dot(rows_q, ent_low.T, preferred_element_type=jnp.float32)  22.6 us
    all_to_all x2, starting transfers between devices, several_exchanges(): lax.all_to_all(slab, axis, split_axis=0, concat_axis=0, tiled=True)  13.4 us
    gather x1, local copies, waits for them, and re-layouts, pick_rows(): picked = jnp.take(table, jnp.clip(local, 0, count - 1), axis=0)  12.9 us
    unnamed x15, local copies, waits for them, and re-layouts  9.66 us
    gather x1, local copies, waits for them, and re-layouts, shards(): jnp.take(relations, rel_ids, axis=0)  8.9 us
  transfers between devices with their start and end apart: 3, of which 1 were waited for; matrix products, arithmetic and copies ran while one was open for 29% of the time, Pallas kernels for 0%

commit v1 on v0

--- a/solution.py
+++ b/solution.py
@@ -50,7 +50,7 @@
     serving = several_exchanges(entity_table, "dim", 2, 1, 0)
     start = (lax.axis_index("rows") * lax.axis_size("dim") + lax.axis_index("dim")) * local_rows
     partial_value = pick_rows(entity_table, head_ids, start)
-    head_vecs = lax.psum(partial_value, ("rows", "dim"))
+    head_vecs = lax.psum(lax.psum(partial_value, "rows"), "dim")
     query = (head_vecs * jnp.take(relations, rel_ids, axis=0)).astype(jnp.bfloat16)
     ent_low = entity_table.astype(jnp.bfloat16)
     level = jnp.take(thresholds, thr_idx)

time: 351 us -> 420 us (1.20)
  blocking collectives: 81.6 us -> 154 us
  starting transfers between devices: 13.4 us -> 4.66 us
  waiting for transfers between devices: 113 us -> 119 us
    all_to_all x0 -> x1, blocking collectives: none -> 89.1 us  [several_exchanges(): lax.all_to_all(slab, axis, split_axis=0, concat_axis=0, tiled=True)]
    unnamed x1, blocking collectives: 81.6 us -> 64.5 us
    all_to_all x2 -> x1, starting transfers between devices: 13.4 us -> 4.58 us  [several_exchanges(): lax.all_to_all(slab, axis, split_axis=0, concat_axis=0, tiled=True)]
    psum x1 -> x2, waiting for transfers between devices: 113 us -> 119 us  [shards(): head_vecs = lax.psum(lax.psum(partial_value, 'rows'), 'dim')]
    unnamed x15 -> x13, local copies, waits for them, and re-layouts: 9.66 us -> 9.53 us
  transfers between devices with their start and end apart: 3 -> 3, of which waited for: 1 -> 2; matrix products, arithmetic and copies ran while one was open for 29% -> 19% of each run, Pallas kernels for 0% -> 0%
where the time goes in v1:
time: 420 us; the launch traced here: 419 us
  blocking collectives  154 us (37%)
  waiting for transfers between devices  119 us (28%)
  other arithmetic  60 us (14%)
  local copies, waits for them, and re-layouts  44.6 us (11%)
  matrix products  22.6 us (5%)
  between operations  14.2 us (3%)
  starting transfers between devices  4.66 us (1%)
    psum x2, waiting for transfers between devices, shards(): head_vecs = lax.psum(lax.psum(partial_value, 'rows'), 'dim')  119 us
    all_to_all x1, blocking collectives, several_exchanges(): lax.all_to_all(slab, axis, split_axis=0, concat_axis=0, tiled=True)  89.1 us
    unnamed x1, blocking collectives  64.5 us
    select_n x1, other arithmetic, shards(): level = jnp.take(thresholds, thr_idx)  39.8 us
    dot_general x4, matrix products, score_block(): score = jnp.dot(rows_q, ent_low.T, preferred_element_type=jnp.float32)  22.6 us
    gather x1, local copies, waits for them, and re-layouts, pick_rows(): picked = jnp.take(table, jnp.clip(local, 0, count - 1), axis=0)  12.9 us
    unnamed x13, local copies, waits for them, and re-layouts  9.53 us
    gather x1, local copies, waits for them, and re-layouts, shards(): jnp.take(relations, rel_ids, axis=0)  8.91 us
  transfers between devices with their start and end apart: 3, of which 2 were waited for; matrix products, arithmetic and copies ran while one was open for 19% of the time, Pallas kernels for 0%

profile of v1, /device:TPU:1, one launch (start us, length us, event | category | flops | bytes accessed | tf_op | source)
XLA Modules:
  0.0 418.8 jit_solution(5497026439710617307)
XLA Ops:
  7.2 0.0 copy-start
  7.2 0.0 all-reduce.4.cloned.1.call-start
  7.2 0.8 compare_and_fusion.2
  8.1 0.7 fusion.5
  8.8 12.9 %gather_fusion = f32[2048,512]{1,0:T(8,128)} fusion(f32[4096,512]{1,0:T(8,128)} %param.8, s32[2048]{0:T(1024)S(1)} %fusion.5), kind=kCustom, calls=%fused_computation | custom fusion | bytes 8396800 | tf_op jit(solution)/shard_map/jit(_take)/gather | solution.py:42
  21.6 3.9 select_select_fusion
  25.6 0.0 all-reduce.4.cloned.1.call-update
  25.6 8.9 %copy.12 = f32[4096,512]{0,1:T(8,128)} copy(f32[4096,512]{1,0:T(8,128)} %param.8) | data formatting | bytes 16777216 | tf_op args[0]
  34.5 6.3 %fusion.6 = (f32[8,2048,64]{1,2,0:T(8,128)S(1)}, f32[8,2048,64]{1,2,0:T(8,128)}) fusion(f32[8,4096,64]{1,2,0:T(8,128)} %bitcast.87), kind=kLoop, calls=%fused_computation.21 | loop fusion | bytes 16777216 | tf_op jit(solution)/shard_map/split | solution.py:32
  40.8 89.1 %all_to_all.10 = f32[8,2048,64]{1,2,0:T(8,128)} all-to-all(f32[8,2048,64]{1,2,0:T(8,128)S(1)} %get-tuple-element.40), channel_id=1, replica_groups=mesh['rows'=16,'dim'=8] {'dim'}, dimensions={0} | all-to-all | bytes 8388608 | tf_op jit(solution)/shard_map/all_to_all | solution.py:34
  129.8 4.6 %all-to-all-start.1 = ((f32[8,2048,64]{1,2,0:T(8,128)}), f32[8,2048,64]{1,2,0:T(8,128)}, u32[]{:S(2)}, u32[]{:S(2)}) async-start(f32[8,2048,64]{1,2,0:T(8,128)} %get-tuple-element.41), calls=%async_computation.1 | async-start | bytes 8388608 | tf_op jit(solution)/shard_map/all_to_all | solution.py:34
  134.4 0.0 all-reduce.6.cloned.1.call-start
  134.5 72.7 %all-reduce.4.cloned.1.call-done = f32[2048,512]{1,0:T(8,128)} async-done(((f32[2048,512]{1,0:T(8,128)}), f32[2048,512]{1,0:T(8,128)}) %all-reduce.4.cloned.1.call-update) | async-done | bytes 4194320 | tf_op jit(solution)/shard_map/psum | solution.py:53
  207.2 0.0 all-reduce.6.cloned.1.call-update
  207.2 0.0 copy-start.2
  207.3 0.0 copy-start.4
  207.3 0.0 copy-start.3
  207.3 5.9 %convert_element_type.7 = bf16[4096,512]{1,0:T(8,128)(2,1)} convert(f32[4096,512]{1,0:T(8,128)} %param.8) | non-fusion elementwise | flops 2097152 | bytes 12582912 | tf_op jit(solution)/shard_map/convert_element_type | solution.py:55
  213.2 0.0 copy-done.2
  213.2 0.7 fusion.10
  213.9 0.7 fusion.8
  214.6 0.7 fusion.7
  215.3 0.7 fusion.9
  216.1 0.0 copy-done.4
  216.1 39.8 %select_select_fusion.1 = f32[2048]{0:T(1024)S(1)} fusion(s32[2048]{0:T(1024)S(1)} %copy-done.4, f32[]{:T(128)} %bitcast.7, f32[]{:T(128)} %bitcast.8, f32[]{:T(128)} %bitcast.9, f32[]{:T(128)} %bitcast.10, f32[]{:T(128)} %bitcast.11, f32[]{:T(128)} %bitcast.12, f32[]{:T(128)} %bitcast.13, f32[]{:T(128)} %bitcast.14, f32[]{:T(128)} %bitcast.15, f32[]{:T(128)} %bitcast.16, ...), kind=kLoop, calls=%fused_computation.15 | loop fusion | flops 272384 | bytes 16640 | tf_op jit(solution)/shard_map/jit(_take)/select_n | solution.py:56
  255.9 0.0 copy-done.3
  255.9 0.0 copy-done
  255.9 8.9 %gather_fusion.1 = f32[2048,512]{1,0:T(8,128)} fusion(f32[822,512]{1,0:T(8,128)S(1)} %copy-done, s32[2048]{0:T(1024)S(1)} %fusion.4), kind=kCustom, calls=%fused_computation.1 | custom fusion | bytes 8396800 | tf_op jit(solution)/shard_map/jit(_take)/gather | solution.py:54
  264.9 0.0 all-to-all-done.1
  264.9 4.0 maximum_bitcast_fusion
  268.9 3.9 copy.14
  272.8 46.3 %all-reduce.6.cloned.1.call-done = f32[2048,512]{1,0:T(8,128)} async-done(((f32[2048,512]{1,0:T(8,128)}), f32[2048,512]{1,0:T(8,128)}) %all-reduce.6.cloned.1.call-update) | async-done | bytes 4194320 | tf_op jit(solution)/shard_map/psum | solution.py:53
  319.1 4.8 %multiply_convert_fusion = bf16[2048,512]{1,0:T(8,128)(2,1)} fusion(f32[2048,512]{1,0:T(8,128)} %all-reduce.6.cloned.1.call-done, f32[2048,512]{1,0:T(8,128)} %gather_fusion.1, pred[2048]{0:T(1024)(128)(4,1)S(1)} %compare_and_fusion), kind=kLoop, calls=%fused_computation.10 | loop fusion | flops 3145728 | bytes 10487808 | tf_op jit(solution)/shard_map/convert_element_type | solution.py:54
  323.9 22.9 %while.10 = (s32[]{:T(128)}, f32[4,512]{1,0:T(4,128)S(1)}, bf16[4,512,512]{2,1,0:T(8,128)(2,1)}, bf16[4096,512]{1,0:T(8,128)(2,1)}, f32[4,512]{1,0:T(4,128)S(1)}, /*index=5*/s32[]{:T(128)}, s32[]{:T(128)}) while((s32[]{:T(128)}, f32[4,512]{1,0:T(4,128)S(1)}, bf16[4,512,512]{2,1,0:T(8,128)(2,1)}, bf16[4096,512]{1,0:T(8,128)(2,1)}, ...), condition=%wide.region_4.5_spmd, body=%wide.region_2.4_spmd.sunk | while | flops 2160066560 | bytes 4735073 | solution.py:67
  323.9 5.6 %fusion.17 = f32[512]{0:T(512)S(1)} fusion(bf16[4096,512]{1,0:T(8,128)(2,1)} %get-tuple-element.156, f32[512]{0:T(512)S(1)} %bitcast.91, bf16[4,512,512]{2,1,0:T(8,128)(2,1)} %get-tuple-element.155, s32[]{:T(128)S(6)} %copy.21), kind=kOutput, calls=%fused_computation.3.clone.1 | convolution fusion | flops 2160066048 | bytes 4722692 | tf_op jit(solution)/shard_map/while/body/eval_jaxpr/dot_general | solution.py:63
  329.6 0.1 dynamic_update_slice.5
  329.7 5.6 %fusion.17 = f32[512]{0:T(512)S(1)} fusion(bf16[4096,512]{1,0:T(8,128)(2,1)} %get-tuple-element.156, f32[512]{0:T(512)S(1)} %bitcast.91, bf16[4,512,512]{2,1,0:T(8,128)(2,1)} %get-tuple-element.155, s32[]{:T(128)S(6)} %copy.21), kind=kOutput, calls=%fused_computation.3.clone.1 | convolution fusion | flops 2160066048 | bytes 4722692 | tf_op jit(solution)/shard_map/while/body/eval_jaxpr/dot_general | solution.py:63
  335.3 0.1 dynamic_update_slice.5
  335.4 5.6 %fusion.17 = f32[512]{0:T(512)S(1)} fusion(bf16[4096,512]{1,0:T(8,128)(2,1)} %get-tuple-element.156, f32[512]{0:T(512)S(1)} %bitcast.91, bf16[4,512,512]{2,1,0:T(8,128)(2,1)} %get-tuple-element.155, s32[]{:T(128)S(6)} %copy.21), kind=kOutput, calls=%fused_computation.3.clone.1 | convolution fusion | flops 2160066048 | bytes 4722692 | tf_op jit(solution)/shard_map/while/body/eval_jaxpr/dot_general | solution.py:63
  341.0 0.1 dynamic_update_slice.5
  341.1 5.6 %fusion.17 = f32[512]{0:T(512)S(1)} fusion(bf16[4096,512]{1,0:T(8,128)(2,1)} %get-tuple-element.156, f32[512]{0:T(512)S(1)} %bitcast.91, bf16[4,512,512]{2,1,0:T(8,128)(2,1)} %get-tuple-element.155, s32[]{:T(128)S(6)} %copy.21), kind=kOutput, calls=%fused_computation.3.clone.1 | convolution fusion | flops 2160066048 | bytes 4722692 | tf_op jit(solution)/shard_map/while/body/eval_jaxpr/dot_general | solution.py:63
  346.8 0.1 dynamic_update_slice.5
  346.8 0.0 copy-start.1
  346.9 64.5 %all-reduce = f32[2048]{0:T(1024)S(1)} all-reduce(f32[2048]{0:T(1024)S(1)} %bitcast.92), channel_id=2, replica_groups=mesh['rows'=16,'dim'=8] {'rows','dim'}, use_global_device_ids=true, to_apply=%region_5.6.clone | all-reduce | flops 2048 | bytes 16384
  411.3 0.6 dynamic-slice
  411.9 0.0 copy-done.1
  (13 shorter events, 0.1 us)
Async XLA Ops:
  7.2 248.8 %copy-start = (f32[822,512]{1,0:T(8,128)S(1)}, f32[822,512]{1,0:T(8,128)}, u32[]{:S(2)}) copy-start(f32[822,512]{1,0:T(8,128)} %param.9) | copy-start | bytes 5050372
  7.2 200.0 %all-reduce.4.cloned.1.call-start = ((), (), s32[]{:S(2)}) async-start(), calls=%async_computation.2 | async-start | bytes 8388608 | tf_op jit(solution)/shard_map/psum | solution.py:53
  129.8 135.0 %all-to-all-start.1 = ((f32[8,2048,64]{1,2,0:T(8,128)}), f32[8,2048,64]{1,2,0:T(8,128)}, u32[]{:S(2)}, u32[]{:S(2)}) async-start(f32[8,2048,64]{1,2,0:T(8,128)} %get-tuple-element.41), calls=%async_computation.1 | async-start | bytes 8388608 | tf_op jit(solution)/shard_map/all_to_all | solution.py:34
  134.4 184.7 %all-reduce.6.cloned.1.call-start = ((), (), s32[]{:S(2)}) async-start(), calls=%async_computation.3 | async-start | bytes 8388608 | tf_op jit(solution)/shard_map/psum | solution.py:53
  207.2 6.0 %copy-start.2 = (f32[64]{0:T(128)S(1)}, f32[64]{0:T(128)}, u32[]{:S(2)}) copy-start(f32[64]{0:T(128)} %param.10) | copy-start | bytes 772
  207.3 8.8 %copy-start.4 = (s32[2048]{0:T(1024)S(1)}, s32[2048]{0:T(1024)}, u32[]{:S(2)}) copy-start(s32[2048]{0:T(1024)} %param.13) | copy-start | bytes 24580
  207.3 48.6 %copy-start.3 = (s32[2048]{0:T(1024)S(1)}, s32[2048]{0:T(1024)}, u32[]{:S(2)}) copy-start(s32[2048]{0:T(1024)} %param.12) | copy-start | bytes 24580
  346.8 65.1 %copy-start.1 = (f32[822,512]{1,0:T(8,128)S(1)}, f32[822,512]{1,0:T(8,128)}, u32[]{:S(2)}) copy-start(f32[822,512]{1,0:T(8,128)} %param.9) | copy-start | bytes 5050372
Sparse Core Ops, SparseCore 0:
  25.7 181.4 all-reduce.3
  209.7 109.3 all-reduce.5
